TPU v7x, 32 devices: a whole 2x2x4 slice. The times are simulated.
32 devices in a mesh: rep: 4 (over y, x), dom: 8 (over z, core).
Axes of the slice: x: 2, y: 2, z: 4, core: 2. Of those that a mesh axis runs over, the one named last changes fastest.
Arguments:
- node_pos: float32 [3, 16384], P(None, 'dom'), may hold values from -6 to 6
- node_order: int32 [8, 2048], P('dom'), may hold values from 0 to 2047, each once within a row
- facet_centroid: float32 [3, 16384], P(None, 'dom'), may hold values from -6 to 6
- facet_normal: float32 [3, 16384], P(None, 'dom'), may hold values from -6 to 6
- facet_nodes: int32 [3, 16384], P(None, 'dom'), may hold values from 0 to 2047
- pair_bucket: int32 [4, 8, 128], P('rep', 'dom'), may hold values from 0 to 15
- pair_owner: int32 [4, 8, 128, 1], P('rep', 'dom'), may hold values from 0 to 7; in each aligned block of 128 rows (0 to 127, 128 to 255, ..., all dimensions but the last counted through in order) at most 32 rows name the same one
- pair_slot: int32 [4, 8, 128], P('rep', 'dom'), may hold values from 0 to 15
- pair_count: int32 [4, 8], P('rep', 'dom'), may hold values from 64 to 128, as said below
Outputs:
- node_force: float32 [3, 16384], P(None, 'dom')
Inputs may be any that keep to these rules, and one draw needn't show every extreme that they name: `pair_owner`: among the 128 pairs of one device, each domain is named at most 32 times, and exactly 32 times in some device's pairs. `pair_count`: some device uses all 128 pairs. `node_order`: each row is a permutation.
All inputs are finite; a program needn't handle non-finite values.
Results may differ from a plain program's by a relative error of at most 0.00013.
Values sent between devices are 32-bit elements; how exact they have to be, the bound alone decides.
A program may use at most 64 MiB of HBM per device.

v0:
```python
import jax
import jax.numpy as jnp
from jax import lax
from jax.sharding import PartitionSpec as P

BUCKET = 128
PAIRS_DEV = 128
STIFFNESS = 0.125
RADIUS_SQ = 4.0
pair_block = 8


def tile_terms(facet_geom, node_points):
    centre = facet_geom[:, 0:3]
    normal = facet_geom[:, 3:6]
    delta = node_points[:, :, None, :] - centre[:, :, :, None]
    gap = jnp.sum(normal[:, :, :, None] * delta, axis=1)
    dist = jnp.sum(delta * delta, axis=1)
    strength = STIFFNESS * jax.nn.softplus(-gap) * jnp.exp(-dist / RADIUS_SQ)
    node_term = jnp.einsum("bkf,bfp->bkp", normal, strength, precision=lax.Precision.HIGHEST)
    reaction = -normal * jnp.sum(strength, axis=2)[:, None, :]
    return (node_term, reaction)


def slot_numbers(owners, is_live, per_owner, dummy_slot):
    rows = owners.shape[0]
    positions = jnp.arange(rows, dtype=jnp.int32)
    earlier = (
        (positions[None, :] < positions[:, None])
        & (owners[None, :] == owners[:, None])
        & is_live[None, :]
    )
    ranking = jnp.sum(earlier.astype(jnp.int32), axis=1)
    return jnp.where(is_live, owners * per_owner + ranking, dummy_slot)


def pair_loop(
    live_count, geom_rows, point_rows, slot_index, bucket_index, is_live, slot_total, bucket_total
):
    width = geom_rows.shape[2]
    geom_pad = jnp.concatenate([geom_rows, jnp.zeros((pair_block, 6, width), jnp.float32)], 0)
    point_pad = jnp.concatenate([point_rows, jnp.zeros((pair_block, 3, width), jnp.float32)], 0)
    slot_pad = jnp.concatenate([slot_index, jnp.full((pair_block,), slot_total, jnp.int32)])
    bucket_pad = jnp.concatenate([bucket_index, jnp.zeros((pair_block,), jnp.int32)])
    live_pad = jnp.concatenate([is_live, jnp.zeros((pair_block,), jnp.bool_)])

    def step(block_index, carry):
        slot_acc, bucket_acc = carry
        start = block_index * pair_block
        facet_geom = lax.dynamic_slice_in_dim(geom_pad, start, pair_block)
        node_points = lax.dynamic_slice_in_dim(point_pad, start, pair_block)
        slot_take = lax.dynamic_slice_in_dim(slot_pad, start, pair_block)
        bucket_take = lax.dynamic_slice_in_dim(bucket_pad, start, pair_block)
        weight = lax.dynamic_slice_in_dim(live_pad, start, pair_block).astype(jnp.float32)
        node_term, reaction = tile_terms(facet_geom, node_points)
        slot_acc = slot_acc.at[slot_take].add(node_term * weight[:, None, None])
        bucket_acc = bucket_acc.at[bucket_take].add(reaction * weight[:, None, None])
        return (slot_acc, bucket_acc)

    blocks = (live_count + pair_block - 1) // pair_block
    start_acc = (
        jnp.zeros((slot_total + 1, 3, width), jnp.float32),
        jnp.zeros((bucket_total, 3, width), jnp.float32),
    )
    return lax.fori_loop(jnp.int32(0), blocks, step, start_acc)


def per_device(
    node_pos,
    node_order,
    facet_centroid,
    facet_normal,
    facet_nodes,
    pair_bucket,
    pair_owner,
    pair_slot,
    pair_count,
):
    domains = lax.axis_size("dom")
    per_owner = max(2, 2 * PAIRS_DEV // domains)
    slot_total = domains * per_owner
    width = BUCKET
    node_buckets = node_pos.shape[1] // width
    facet_buckets = facet_centroid.shape[1] // width
    bucket_points = node_pos[:, node_order[0]].reshape(3, node_buckets, width).transpose(1, 0, 2)
    bucket_geom = (
        jnp.concatenate([facet_centroid, facet_normal], 0)
        .reshape(6, facet_buckets, width)
        .transpose(1, 0, 2)
    )
    owners = pair_owner[0, 0, :, 0]
    buckets = pair_bucket[0, 0]
    slots = pair_slot[0, 0]
    rows = buckets.shape[0]
    positions = jnp.arange(rows, dtype=jnp.int32)
    is_live = positions < pair_count[0, 0]
    live_count = jnp.sum(is_live.astype(jnp.int32))
    slot_index = slot_numbers(owners, is_live, per_owner, slot_total)
    request = (
        jnp.full((slot_total + 1,), -1, jnp.int32)
        .at[slot_index]
        .set(slots)[:-1]
        .reshape(domains, per_owner)
    )
    every_bucket = lax.all_gather(bucket_points, "dom", axis=0, tiled=True)
    point_rows = every_bucket[owners * node_buckets + slots]
    slot_acc, facet_acc = pair_loop(
        live_count,
        bucket_geom[buckets],
        point_rows,
        slot_index,
        buckets,
        is_live,
        slot_total,
        facet_buckets,
    )
    home_blocks, home_slots = (
        lax.all_to_all(
            slot_acc[:-1].reshape(domains, per_owner, 3, width),
            "dom",
            split_axis=0,
            concat_axis=0,
            tiled=True,
        ),
        lax.all_to_all(request.astype(jnp.float32), "dom", split_axis=0, concat_axis=0, tiled=True),
    )
    home_slots = home_slots.reshape(slot_total).astype(jnp.int32)
    home_blocks = home_blocks.reshape(slot_total, 3, width)
    target = jnp.where(home_slots >= 0, home_slots, node_buckets)
    bucket_force = (
        jnp.zeros((node_buckets + 1, 3, width), jnp.float32).at[target].add(home_blocks)[:-1]
    )
    node_force = (
        jnp.zeros((3, node_pos.shape[1]), jnp.float32)
        .at[:, node_order[0]]
        .add(bucket_force.transpose(1, 0, 2).reshape(3, -1))
    )
    reaction = facet_acc.transpose(1, 0, 2).reshape(3, -1) / 3.0
    for corner in range(3):
        node_force = node_force.at[:, facet_nodes[corner]].add(reaction)
    return lax.psum(node_force, "rep")


def solution(mesh):
    placed = (
        P(None, "dom"),
        P("dom", None),
        P(None, "dom"),
        P(None, "dom"),
        P(None, "dom"),
        P("rep", "dom", None),
        P("rep", "dom", None, None),
        P("rep", "dom", None),
        P("rep", "dom"),
    )
    return jax.shard_map(
        per_device, mesh=mesh, in_specs=placed, out_specs=P(None, "dom"), check_vma=False
    )
```

profile of v0, /device:TPU:0, one launch (start us, length us, event | category | flops | bytes accessed | tf_op | source)
XLA Modules:
  0.0 215.3 jit_solution(11657129899521065713)
XLA Ops:
  0.7 0.9 convert_reduce_fusion
  2.3 1.1 scatter_custom_fusion.2
  4.1 6.4 %all-to-all-start = ((f32[8,1,32]{2,1,0:T(1,128)}), f32[8,1,32]{2,1,0:T(1,128)S(1)}, u32[]{:S(2)}, u32[]{:S(2)}) async-start(f32[8,1,32]{2,1,0:T(1,128)} %convert_element_type.37), calls=%async_computation | async-start | bytes 8192 | tf_op jit(solution)/shard_map/all_to_all | solution.py:125
  12.4 1.1 copy.46
  13.5 5.5 %gather_fusion.1 = f32[2048,3]{1,0:T(8,128)S(1)} fusion(f32[3,2048]{0,1:T(8,128)S(1)} %copy.46, s32[2048]{0:T(1024)S(1)} %broadcast_clamp_fusion), kind=kCustom, calls=%fused_computation.1 | custom fusion | bytes 57344 | tf_op jit(solution)/shard_map/gather | solution.py:85
  19.3 14.8 %all_gather.3 = f32[128,3,128]{2,0,1:T(8,128)S(1)} all-gather(f32[16,3,128]{2,0,1:T(8,128)S(1)} %bitcast.77), channel_id=1, replica_groups=mesh['rep'=4,'dom'=8] {'dom'}, dimensions={0}, use_global_device_ids=true | all-gather | bytes 221184 | tf_op jit(solution)/shard_map/all_gather | solution.py:105
  36.1 62.5 %while.12 = (s32[]{:T(128)}, f32[257,3,128]{2,1,0:T(4,128)S(1)}, f32[16,3,128]{2,1,0:T(4,128)S(1)}, s32[]{:T(128)}, s32[136]{0:T(256)S(1)}, /*index=5*/f32[136,6...) while((s32[]{:T(128)}, f32[257,3,128]{2,1,0:T(4,128)S(1)}, ...), condition=%wide.region_9.10_spmd, body=%wide.region_3.9_spmd.sunk | while | flops 8012863 | bytes 3387895 | solution.py:65
  36.1 1.0 fusion.23
  38.3 0.8 scatter_fusion
  39.2 0.8 scatter_fusion.1
  40.1 1.0 fusion.23
  42.3 0.8 scatter_fusion
  43.1 0.8 scatter_fusion.1
  44.0 1.0 fusion.23
  46.2 0.8 scatter_fusion
  47.0 0.8 scatter_fusion.1
  47.9 1.0 fusion.23
  50.1 0.8 scatter_fusion
  50.9 0.8 scatter_fusion.1
  51.8 1.0 fusion.23
  54.0 0.8 scatter_fusion
  54.8 0.8 scatter_fusion.1
  55.7 1.0 fusion.23
  57.9 0.8 scatter_fusion
  58.7 0.8 scatter_fusion.1
  59.6 1.0 fusion.23
  61.8 0.8 scatter_fusion
  62.6 0.8 scatter_fusion.1
  63.5 1.0 fusion.23
  65.7 0.8 scatter_fusion
  66.5 0.8 scatter_fusion.1
  67.4 1.0 fusion.23
  69.6 0.8 scatter_fusion
  70.5 0.8 scatter_fusion.1
  71.3 1.0 fusion.23
  73.5 0.8 scatter_fusion
  74.4 0.8 scatter_fusion.1
  75.2 1.0 fusion.23
  77.4 0.8 scatter_fusion
  78.3 0.8 scatter_fusion.1
  79.1 1.0 fusion.23
  81.3 0.8 scatter_fusion
  82.2 0.8 scatter_fusion.1
  83.0 1.0 fusion.23
  85.2 0.8 scatter_fusion
  86.1 0.8 scatter_fusion.1
  86.9 1.0 fusion.23
  89.1 0.8 scatter_fusion
  90.0 0.8 scatter_fusion.1
  90.8 1.0 fusion.23
  93.0 0.8 scatter_fusion
  93.9 0.8 scatter_fusion.1
  94.7 1.0 fusion.23
  96.9 0.8 scatter_fusion
  97.8 0.8 scatter_fusion.1
  99.8 3.5 %all-to-all-start.1 = ((f32[8,32,3,128]{3,1,2,0:T(8,128)}), f32[8,32,3,128]{3,1,2,0:T(8,128)S(1)}, u32[]{:S(2)}, u32[]{:S(2)}) async-start(f32[8,32,3,128]{3,1,2,0:T(8,128)} %copy.50), calls=%async_computation.1 | async-start | bytes 786432 | tf_op jit(solution)/shard_map/all_to_all | solution.py:118
  103.5 12.3 %all-to-all-done.1 = f32[8,32,3,128]{3,1,2,0:T(8,128)S(1)} async-done(((f32[8,32,3,128]{3,1,2,0:T(8,128)}), f32[8,32,3,128]{3,1,2,0:T(8,128)S(1)}, u32[]{:S(2)}, u32[]{:S(2)}) %all-to-all-start.1) | async-done | bytes 393248 | tf_op jit(solution)/shard_map/all_to_all | solution.py:118
  116.1 8.9 %scatter_fusion.2 = f32[17,3,128]{2,1,0:T(4,128)S(1)} fusion(f32[17,3,128]{2,1,0:T(4,128)S(1)} %broadcast_in_dim.32, s32[256]{0:T(256)S(1)} %bitcast.84, f32[256,3,128]{2,1,0:T(4,128)S(1)} %copy.52), kind=kCustom, calls=%fused_computation.6 | custom fusion | flops 98304 | bytes 1180672 | tf_op jit(solution)/shard_map/scatter-add | solution.py:131
  125.3 11.7 %scatter_custom_fusion.4 = f32[3,2048]{0,1:T(8,128)S(1)} fusion(s32[2048]{0:T(1024)S(1)} %bitcast.82, f32[2048,3]{1,0:T(8,128)S(1)} %copy.53, f32[]{:T(128)} %constant.33.clone.1), kind=kCustom, calls=%fused_computation.26 | custom fusion | flops 6144 | bytes 24580 | tf_op jit(solution)/shard_map/scatter-add | solution.py:136
  137.1 11.9 %scatter_fusion.3 = f32[3,2048]{0,1:T(8,128)S(1)} fusion(f32[3,2048]{0,1:T(8,128)S(1)} %scatter_custom_fusion.4, s32[2048]{0:T(1024)S(1)} %bitcast.80, f32[2048,3]{1,0:T(8,128)S(1)} %copy.54), kind=kCustom, calls=%fused_computation.8 | custom fusion | flops 6144 | bytes 81920 | tf_op jit(solution)/shard_map/scatter-add | solution.py:140
  148.9 12.1 %scatter_fusion.4 = f32[3,2048]{0,1:T(8,128)S(1)} fusion(f32[3,2048]{0,1:T(8,128)S(1)} %scatter_fusion.3, s32[2048]{0:T(1024)S(1)} %bitcast.79, f32[2048,3]{1,0:T(8,128)S(1)} %copy.54), kind=kCustom, calls=%fused_computation.9 | custom fusion | flops 6144 | bytes 81920 | tf_op jit(solution)/shard_map/scatter-add | solution.py:140
  161.0 11.9 %scatter_fusion.5 = f32[3,2048]{0,1:T(8,128)S(1)} fusion(f32[3,2048]{0,1:T(8,128)S(1)} %scatter_fusion.4, s32[2048]{0:T(1024)S(1)} %bitcast.78, f32[2048,3]{1,0:T(8,128)S(1)} %copy.54), kind=kCustom, calls=%fused_computation.10 | custom fusion | flops 6144 | bytes 81920 | tf_op jit(solution)/shard_map/scatter-add | solution.py:140
  172.9 41.5 %psum.7 = f32[3,2048]{0,1:T(8,128)S(1)} all-reduce(f32[3,2048]{0,1:T(8,128)S(1)} %scatter_fusion.5), channel_id=1, replica_groups=mesh['rep'=4,'dom'=8] {'rep'}, use_global_device_ids=true, to_apply=%region_15.16 | all-reduce | flops 6144 | bytes 49152 | tf_op jit(solution)/shard_map/psum | solution.py:141
  214.4 0.9 copy.57
  (144 shorter events, 26.9 us)
Async XLA Ops:
  4.1 95.8 %all-to-all-start = ((f32[8,1,32]{2,1,0:T(1,128)}), f32[8,1,32]{2,1,0:T(1,128)S(1)}, u32[]{:S(2)}, u32[]{:S(2)}) async-start(f32[8,1,32]{2,1,0:T(1,128)} %convert_element_type.37), calls=%async_computation | async-start | bytes 8192 | tf_op jit(solution)/shard_map/all_to_all | solution.py:125
  13.5 20.7 %copy-start.3 = (s32[1,1,128,1]{2,3,1,0:T(1,128)S(1)}, s32[1,1,128,1]{2,3,1,0:T(1,128)}, u32[]{:S(2)}) copy-start(s32[1,1,128,1]{2,3,1,0:T(1,128)} %param.17) | copy-start | bytes 1540
  13.5 20.8 %copy-start.4 = (s32[1,1,128]{2,1,0:T(1,128)S(1)}, s32[1,1,128]{2,1,0:T(1,128)}, u32[]{:S(2)}) copy-start(s32[1,1,128]{2,1,0:T(1,128)} %param.16) | copy-start | bytes 1540
  19.3 15.8 %copy-start = (f32[3,2048]{1,0:T(4,128)S(1)}, f32[3,2048]{1,0:T(4,128)}, u32[]{:S(2)}) copy-start(f32[3,2048]{1,0:T(4,128)} %param.14) | copy-start | bytes 73732
  19.3 15.8 %copy-start.1 = (f32[3,2048]{1,0:T(4,128)S(1)}, f32[3,2048]{1,0:T(4,128)}, u32[]{:S(2)}) copy-start(f32[3,2048]{1,0:T(4,128)} %param.13) | copy-start | bytes 73732
  99.5 3.9 %copy-start.2 = (s32[3,2048]{1,0:T(4,128)S(1)}, s32[3,2048]{1,0:T(4,128)}, u32[]{:S(2)}) copy-start(s32[3,2048]{1,0:T(4,128)} %param.15) | copy-start | bytes 73732
  99.8 15.9 %all-to-all-start.1 = ((f32[8,32,3,128]{3,1,2,0:T(8,128)}), f32[8,32,3,128]{3,1,2,0:T(8,128)S(1)}, u32[]{:S(2)}, u32[]{:S(2)}) async-start(f32[8,32,3,128]{3,1,2,0:T(8,128)} %copy.50), calls=%async_computation.1 | async-start | bytes 786432 | tf_op jit(solution)/shard_map/all_to_all | solution.py:118
where the time goes:
time: 216 us; the launch traced here: 215 us
  other arithmetic  112 us (52%)
  blocking collectives  56.2 us (26%)
  local copies, waits for them, and re-layouts  13.8 us (6%)
  waiting for transfers between devices  12.3 us (6%)
  starting transfers between devices  9.82 us (5%)
  matrix products  8.35 us (4%)
    psum x1, blocking collectives, per_device(): return lax.psum(node_force, 'rep')  41.5 us
    scatter-add x3, other arithmetic, per_device(): node_force = node_force.at[:, facet_nodes[corner]].add(reaction)  35.8 us
    reduce_sum x16, other arithmetic, tile_terms(): gap = jnp.sum(normal[:, :, :, None] * delta, axis=1)  16.6 us
    all_gather x1, blocking collectives, per_device(): every_bucket = lax.all_gather(bucket_points, 'dom', axis=0, tiled=True)  14.8 us
    scatter-add x16, other arithmetic, step(): slot_acc = slot_acc.at[slot_take].add(node_term * weight[:, None, None])  12.5 us
    scatter-add x16, other arithmetic, step(): bucket_acc.at[bucket_take].add(reaction * weight[:, None, None])  12.5 us
    all_to_all x1, waiting for transfers between devices, per_device(): lax.all_to_all(slot_acc[:-1].reshape(domains, per_owner, 3, width), 'dom'...  12.3 us
    scatter-add x1, other arithmetic, per_device(): node_force = jnp.zeros((3, node_pos.shape[1]), jnp.float32).at[:, node_or...  11.7 us
  transfers between devices with their start and end apart: 2, of which 1 were waited for; matrix products, arithmetic and copies ran while one was open for 34% of the time, Pallas kernels for 0%

commit v1 on v0

--- a/solution.py
+++ b/solution.py
@@ -138,7 +138,7 @@
     reaction = facet_acc.transpose(1, 0, 2).reshape(3, -1) / 3.0
     for corner in range(3):
         node_force = node_force.at[:, facet_nodes[corner]].add(reaction)
-    return lax.psum(node_force, "rep")
+    return jnp.sum(lax.all_gather(node_force, "rep"), axis=0)
 
 
 def solution(mesh):

time: 216 us -> 184 us (0.85)
  blocking collectives: 56.2 us -> 24.4 us
    psum x1 -> x0, blocking collectives: 41.5 us -> none  [per_device(): return lax.psum(node_force, 'rep')]
    all_gather x0 -> x1, blocking collectives: none -> 9.59 us  [per_device(): return jnp.sum(lax.all_gather(node_force, 'rep'), axis=0)]
  transfers between devices with their start and end apart: 2 -> 2, of which waited for: 1 -> 1; matrix products, arithmetic and copies ran while one was open for 34% -> 40% of each run, Pallas kernels for 0% -> 0%
where the time goes in v1:
time: 184 us; the launch traced here: 183 us
  other arithmetic  113 us (61%)
  blocking collectives  24.4 us (13%)
  local copies, waits for them, and re-layouts  13.1 us (7%)
  waiting for transfers between devices  12.3 us (7%)
  starting transfers between devices  9.82 us (5%)
  matrix products  8.35 us (5%)
    scatter-add x3, other arithmetic, per_device(): node_force = node_force.at[:, facet_nodes[corner]].add(reaction)  35.6 us
    reduce_sum x16, other arithmetic, tile_terms(): gap = jnp.sum(normal[:, :, :, None] * delta, axis=1)  16.6 us
    all_gather x1, blocking collectives, per_device(): every_bucket = lax.all_gather(bucket_points, 'dom', axis=0, tiled=True)  14.8 us
    scatter-add x16, other arithmetic, step(): slot_acc = slot_acc.at[slot_take].add(node_term * weight[:, None, None])  12.5 us
    scatter-add x16, other arithmetic, step(): bucket_acc.at[bucket_take].add(reaction * weight[:, None, None])  12.5 us
    all_to_all x1, waiting for transfers between devices, per_device(): lax.all_to_all(slot_acc[:-1].reshape(domains, per_owner, 3, width), 'dom'...  12.3 us
    scatter-add x1, other arithmetic, per_device(): node_force = jnp.zeros((3, node_pos.shape[1]), jnp.float32).at[:, node_or...  11.7 us
    all_gather x1, blocking collectives, per_device(): return jnp.sum(lax.all_gather(node_force, 'rep'), axis=0)  9.59 us
  transfers between devices with their start and end apart: 2, of which 1 were waited for; matrix products, arithmetic and copies ran while one was open for 40% of the time, Pallas kernels for 0%

profile of v1, /device:TPU:0, one launch (start us, length us, event | category | flops | bytes accessed | tf_op | source)
XLA Modules:
  0.0 183.3 jit_solution(5086986562550528832)
XLA Ops:
  0.7 0.9 convert_reduce_fusion
  2.3 1.1 scatter_custom_fusion.2
  4.1 6.4 %all-to-all-start = ((f32[8,1,32]{2,1,0:T(1,128)}), f32[8,1,32]{2,1,0:T(1,128)S(1)}, u32[]{:S(2)}, u32[]{:S(2)}) async-start(f32[8,1,32]{2,1,0:T(1,128)} %convert_element_type.37), calls=%async_computation | async-start | bytes 8192 | tf_op jit(solution)/shard_map/all_to_all | solution.py:125
  12.4 1.1 copy.47
  13.5 5.5 %gather_fusion.1 = f32[2048,3]{1,0:T(8,128)S(1)} fusion(f32[3,2048]{0,1:T(8,128)S(1)} %copy.47, s32[2048]{0:T(1024)S(1)} %broadcast_clamp_fusion), kind=kCustom, calls=%fused_computation.1 | custom fusion | bytes 57344 | tf_op jit(solution)/shard_map/gather | solution.py:85
  19.3 14.8 %all_gather.9 = f32[128,3,128]{2,0,1:T(8,128)S(1)} all-gather(f32[16,3,128]{2,0,1:T(8,128)S(1)} %bitcast.79), channel_id=1, replica_groups=mesh['rep'=4,'dom'=8] {'dom'}, dimensions={0}, use_global_device_ids=true | all-gather | bytes 221184 | tf_op jit(solution)/shard_map/all_gather | solution.py:105
  36.1 62.5 %while.12 = (s32[]{:T(128)}, f32[257,3,128]{2,1,0:T(4,128)S(1)}, f32[16,3,128]{2,1,0:T(4,128)S(1)}, s32[]{:T(128)}, s32[136]{0:T(256)S(1)}, /*index=5*/f32[136,6...) while((s32[]{:T(128)}, f32[257,3,128]{2,1,0:T(4,128)S(1)}, ...), condition=%wide.region_9.10_spmd, body=%wide.region_3.9_spmd.sunk | while | flops 8012863 | bytes 3387895 | solution.py:65
  36.1 1.0 fusion.23
  38.3 0.8 scatter_fusion
  39.2 0.8 scatter_fusion.1
  40.1 1.0 fusion.23
  42.3 0.8 scatter_fusion
  43.1 0.8 scatter_fusion.1
  44.0 1.0 fusion.23
  46.2 0.8 scatter_fusion
  47.0 0.8 scatter_fusion.1
  47.9 1.0 fusion.23
  50.1 0.8 scatter_fusion
  50.9 0.8 scatter_fusion.1
  51.8 1.0 fusion.23
  54.0 0.8 scatter_fusion
  54.8 0.8 scatter_fusion.1
  55.7 1.0 fusion.23
  57.9 0.8 scatter_fusion
  58.7 0.8 scatter_fusion.1
  59.6 1.0 fusion.23
  61.8 0.8 scatter_fusion
  62.6 0.8 scatter_fusion.1
  63.5 1.0 fusion.23
  65.7 0.8 scatter_fusion
  66.5 0.8 scatter_fusion.1
  67.4 1.0 fusion.23
  69.6 0.8 scatter_fusion
  70.5 0.8 scatter_fusion.1
  71.3 1.0 fusion.23
  73.5 0.8 scatter_fusion
  74.4 0.8 scatter_fusion.1
  75.2 1.0 fusion.23
  77.4 0.8 scatter_fusion
  78.3 0.8 scatter_fusion.1
  79.1 1.0 fusion.23
  81.3 0.8 scatter_fusion
  82.2 0.8 scatter_fusion.1
  83.0 1.0 fusion.23
  85.2 0.8 scatter_fusion
  86.1 0.8 scatter_fusion.1
  86.9 1.0 fusion.23
  89.1 0.8 scatter_fusion
  90.0 0.8 scatter_fusion.1
  90.8 1.0 fusion.23
  93.0 0.8 scatter_fusion
  93.9 0.8 scatter_fusion.1
  94.7 1.0 fusion.23
  96.9 0.8 scatter_fusion
  97.8 0.8 scatter_fusion.1
  98.7 0.8 copy.51
  99.8 3.5 %all-to-all-start.1 = ((f32[8,32,3,128]{3,1,2,0:T(8,128)}), f32[8,32,3,128]{3,1,2,0:T(8,128)S(1)}, u32[]{:S(2)}, u32[]{:S(2)}) async-start(f32[8,32,3,128]{3,1,2,0:T(8,128)} %copy.51), calls=%async_computation.1 | async-start | bytes 786432 | tf_op jit(solution)/shard_map/all_to_all | solution.py:118
  103.5 12.3 %all-to-all-done.1 = f32[8,32,3,128]{3,1,2,0:T(8,128)S(1)} async-done(((f32[8,32,3,128]{3,1,2,0:T(8,128)}), f32[8,32,3,128]{3,1,2,0:T(8,128)S(1)}, u32[]{:S(2)}, u32[]{:S(2)}) %all-to-all-start.1) | async-done | bytes 393248 | tf_op jit(solution)/shard_map/all_to_all | solution.py:118
  116.1 8.9 %scatter_fusion.2 = f32[17,3,128]{2,1,0:T(4,128)S(1)} fusion(f32[17,3,128]{2,1,0:T(4,128)S(1)} %broadcast_in_dim.32, s32[256]{0:T(256)S(1)} %bitcast.86, f32[256,3,128]{2,1,0:T(4,128)S(1)} %copy.53), kind=kCustom, calls=%fused_computation.6 | custom fusion | flops 98304 | bytes 1180672 | tf_op jit(solution)/shard_map/scatter-add | solution.py:131
  125.3 11.7 %scatter_custom_fusion.4 = f32[3,2048]{0,1:T(8,128)S(1)} fusion(s32[2048]{0:T(1024)S(1)} %bitcast.84, f32[2048,3]{1,0:T(8,128)S(1)} %copy.54, f32[]{:T(128)} %constant.33.clone.1), kind=kCustom, calls=%fused_computation.26 | custom fusion | flops 6144 | bytes 24580 | tf_op jit(solution)/shard_map/scatter-add | solution.py:136
  137.1 11.9 %scatter_fusion.3 = f32[3,2048]{0,1:T(8,128)S(1)} fusion(f32[3,2048]{0,1:T(8,128)S(1)} %scatter_custom_fusion.4, s32[2048]{0:T(1024)S(1)} %bitcast.82, f32[2048,3]{1,0:T(8,128)S(1)} %copy.55), kind=kCustom, calls=%fused_computation.8 | custom fusion | flops 6144 | bytes 81920 | tf_op jit(solution)/shard_map/scatter-add | solution.py:140
  148.9 11.9 %scatter_fusion.4 = f32[3,2048]{0,1:T(8,128)S(1)} fusion(f32[3,2048]{0,1:T(8,128)S(1)} %scatter_fusion.3, s32[2048]{0:T(1024)S(1)} %bitcast.81, f32[2048,3]{1,0:T(8,128)S(1)} %copy.55), kind=kCustom, calls=%fused_computation.9 | custom fusion | flops 6144 | bytes 81920 | tf_op jit(solution)/shard_map/scatter-add | solution.py:140
  160.8 11.9 %scatter_fusion.5 = f32[3,2048]{0,1:T(8,128)S(1)} fusion(f32[3,2048]{0,1:T(8,128)S(1)} %scatter_fusion.4, s32[2048]{0:T(1024)S(1)} %bitcast.80, f32[2048,3]{1,0:T(8,128)S(1)} %copy.55), kind=kCustom, calls=%fused_computation.10 | custom fusion | flops 6144 | bytes 81920 | tf_op jit(solution)/shard_map/scatter-add | solution.py:140
  173.0 9.6 %all-gather.1 = f32[4,3,2048]{2,1,0:T(4,128)S(1)} all-gather(f32[1,3,2048]{2,1,0:T(4,128)S(1)} %copy.58), channel_id=2, replica_groups=mesh['rep'=4,'dom'=8] {'rep'}, dimensions={0}, use_global_device_ids=true | all-gather | bytes 122880 | tf_op jit(solution)/shard_map/all_gather | solution.py:141
  (145 shorter events, 27.1 us)
Async XLA Ops:
  4.1 95.8 %all-to-all-start = ((f32[8,1,32]{2,1,0:T(1,128)}), f32[8,1,32]{2,1,0:T(1,128)S(1)}, u32[]{:S(2)}, u32[]{:S(2)}) async-start(f32[8,1,32]{2,1,0:T(1,128)} %convert_element_type.37), calls=%async_computation | async-start | bytes 8192 | tf_op jit(solution)/shard_map/all_to_all | solution.py:125
  13.5 20.7 %copy-start.3 = (s32[1,1,128,1]{2,3,1,0:T(1,128)S(1)}, s32[1,1,128,1]{2,3,1,0:T(1,128)}, u32[]{:S(2)}) copy-start(s32[1,1,128,1]{2,3,1,0:T(1,128)} %param.17) | copy-start | bytes 1540
  13.5 20.8 %copy-start.4 = (s32[1,1,128]{2,1,0:T(1,128)S(1)}, s32[1,1,128]{2,1,0:T(1,128)}, u32[]{:S(2)}) copy-start(s32[1,1,128]{2,1,0:T(1,128)} %param.16) | copy-start | bytes 1540
  19.3 15.8 %copy-start = (f32[3,2048]{1,0:T(4,128)S(1)}, f32[3,2048]{1,0:T(4,128)}, u32[]{:S(2)}) copy-start(f32[3,2048]{1,0:T(4,128)} %param.14) | copy-start | bytes 73732
  19.3 15.8 %copy-start.1 = (f32[3,2048]{1,0:T(4,128)S(1)}, f32[3,2048]{1,0:T(4,128)}, u32[]{:S(2)}) copy-start(f32[3,2048]{1,0:T(4,128)} %param.13) | copy-start | bytes 73732
  99.5 3.9 %copy-start.2 = (s32[3,2048]{1,0:T(4,128)S(1)}, s32[3,2048]{1,0:T(4,128)}, u32[]{:S(2)}) copy-start(s32[3,2048]{1,0:T(4,128)} %param.15) | copy-start | bytes 73732
  99.8 15.9 %all-to-all-start.1 = ((f32[8,32,3,128]{3,1,2,0:T(8,128)}), f32[8,32,3,128]{3,1,2,0:T(8,128)S(1)}, u32[]{:S(2)}, u32[]{:S(2)}) async-start(f32[8,32,3,128]{3,1,2,0:T(8,128)} %copy.51), calls=%async_computation.1 | async-start | bytes 786432 | tf_op jit(solution)/shard_map/all_to_all | solution.py:118
